TPU v7x, 32 devices: a whole 2x2x4 slice. The times are simulated.
32 devices in a mesh: fsdp: 8 (over z, y), dom: 4 (over x, core).
Axes of the slice: x: 2, y: 2, z: 4, core: 2. Of those that a mesh axis runs over, the one named last changes fastest.
Arguments:
- hidden_states: bfloat16 [256, 128, 768], P(('fsdp', 'dom')), may hold values from -40 to 40
- title_tokens: int32 [256, 128], P(('fsdp', 'dom')), may hold values from 0 to 30521, as said below
- query_key_value: bfloat16 [768, 2304], P('fsdp'), may hold values from -0.5 to 2.5
- output_weight: bfloat16 [768, 768], P('fsdp'), may hold values from -0.21875 to 0.21875
- up_weight: bfloat16 [768, 3072], P('fsdp'), may hold values from -0.21875 to 0.21875
- down_weight: bfloat16 [3072, 768], P('fsdp'), may hold values from -0.109375 to 0.109375
- attention_gain: float32 [768], replicated, may hold values from 0.25 to 1.75
- feedforward_gain: float32 [768], replicated, may hold values from 0.25 to 1.75
- encoded: bfloat16 [16384, 768], P(('fsdp', 'dom')), may hold values from -6 to 6
- send_rows: int32 [32, 32, 48], P(('fsdp', 'dom')), may hold values from 0 to 511
- send_count: int32 [32, 32], P(('fsdp', 'dom')), may hold values from 6 to 48, as said below
- arrival_nodes: int32 [32, 32, 48], P(('fsdp', 'dom')), may hold values from 0 to 511
- sage_weight: bfloat16 [2, 768, 1024], P(None, 'fsdp'), may hold values from -0.21875 to 0.21875
- node_gain: float32 [1024], replicated, may hold values from 0.25 to 1.75
Outputs:
- title_vectors: bfloat16 [256, 768], P(('fsdp', 'dom'))
- node_output: bfloat16 [16384, 1024], P(('fsdp', 'dom'))
Inputs may be any that keep to these rules, and one draw needn't show every extreme that they name: `title_tokens`: in each title the nonzero ids come first and zeros fill the rest; at least 16 ids of every title are nonzero. `send_count`: in every draw some device receives exactly 48 valid slots from every device.
All inputs are finite; a program needn't handle non-finite values.
Results may differ from a plain program's by a relative error of at most 0.0056.
Values may be sent and summed in bfloat16 or wider, within the bound.
A program may use at most 192 MiB of HBM per device.

v0:
```python
import math
import jax
import jax.numpy as jnp
from jax import lax
from jax.sharding import PartitionSpec as P

HEADS = 12
HEAD_DIM = 64
LN_EPSILON = 1e-12


def layer_norm(values, gain):
    center = values - jnp.mean(values, axis=-1, keepdims=True)
    spread = jnp.mean(center * center, axis=-1, keepdims=True)
    return center * lax.rsqrt(spread + LN_EPSILON) * gain


def encode_titles(
    hidden_states,
    title_tokens,
    query_key_value,
    output_weight,
    up_weight,
    down_weight,
    attention_gain,
    feedforward_gain,
):
    titles, seq_len, width = hidden_states.shape
    flat = hidden_states.reshape(titles * seq_len, width)
    live = title_tokens != 0
    full_project, full_output = (
        lax.all_gather(query_key_value, "fsdp", axis=0, tiled=True),
        lax.all_gather(output_weight, "fsdp", axis=0, tiled=True),
    )
    projected = jnp.dot(flat, full_project, preferred_element_type=jnp.float32).astype(jnp.bfloat16)
    projected = projected.reshape(titles, seq_len, 3, HEADS, HEAD_DIM)
    query_states = projected[:, :, 0]
    key_states = projected[:, :, 1]
    value_states = projected[:, :, 2]
    scores = jnp.einsum(
        "tihd,tjhd->thij", query_states, key_states, preferred_element_type=jnp.float32
    )
    scores = scores * (1.0 / math.sqrt(HEAD_DIM))
    scores = jnp.where(live[:, None, None, :], scores, -jnp.inf)
    highest = jnp.max(scores, axis=-1, keepdims=True)
    weights = jnp.exp(scores - highest)
    probs = (weights / jnp.sum(weights, axis=-1, keepdims=True)).astype(jnp.bfloat16)
    context = jnp.einsum("thij,tjhd->tihd", probs, value_states, preferred_element_type=jnp.float32)
    context = context.astype(jnp.bfloat16).reshape(titles * seq_len, width)
    mixed = jnp.dot(context, full_output, preferred_element_type=jnp.float32)
    attended = layer_norm(flat.astype(jnp.float32) + mixed, attention_gain).astype(jnp.bfloat16)
    attended = lax.optimization_barrier(attended)
    full_up, full_down = (
        lax.all_gather(up_weight, "fsdp", axis=0, tiled=True),
        lax.all_gather(down_weight, "fsdp", axis=0, tiled=True),
    )
    inner = jax.nn.gelu(
        jnp.dot(attended, full_up, preferred_element_type=jnp.float32), approximate=False
    )
    inner = inner.astype(jnp.bfloat16)
    lowered = jnp.dot(inner, full_down, preferred_element_type=jnp.float32)
    token_out = layer_norm(attended.astype(jnp.float32) + lowered, feedforward_gain).reshape(
        titles, seq_len, width
    )
    live_weight = live.astype(jnp.float32)
    pooled = jnp.sum(token_out * live_weight[:, :, None], axis=1) / jnp.sum(
        live_weight, axis=1, keepdims=True
    )
    return pooled.astype(jnp.bfloat16)


def scatter_sums(arrived, targets, valid, nodes):
    width = arrived.shape[2]
    mask_flat = valid.reshape(-1).astype(jnp.float32)
    label_flat = targets.reshape(-1)
    rows = arrived.reshape(-1, width).astype(jnp.float32) * mask_flat[:, None]
    sums = jax.ops.segment_sum(rows, label_flat, num_segments=nodes)
    degree = jax.ops.segment_sum(mask_flat, label_flat, num_segments=nodes)
    return (sums, degree)


def on_device(
    hidden_states,
    title_tokens,
    query_key_value,
    output_weight,
    up_weight,
    down_weight,
    attention_gain,
    feedforward_gain,
    encoded,
    send_rows,
    send_count,
    arrival_nodes,
    sage_weight,
    node_gain,
):
    titles = hidden_states.shape[0]
    nodes, width = encoded.shape
    outgoing = jnp.take(encoded, send_rows[0], axis=0)
    slot_count = outgoing.shape[1]
    counts_out = send_count[0].astype(jnp.bfloat16)
    arrived, arrived_counts = (
        lax.all_to_all(outgoing, ("fsdp", "dom"), split_axis=0, concat_axis=0, tiled=True),
        lax.all_to_all(counts_out, ("fsdp", "dom"), split_axis=0, concat_axis=0, tiled=True),
    )
    valid = (
        jnp.arange(slot_count, dtype=jnp.int32)[None, :] < arrived_counts.astype(jnp.int32)[:, None]
    )
    targets = arrival_nodes[0]
    title_vectors = encode_titles(
        hidden_states,
        title_tokens,
        query_key_value,
        output_weight,
        up_weight,
        down_weight,
        attention_gain,
        feedforward_gain,
    )
    sums, degree = scatter_sums(arrived, targets, valid, nodes)
    neighbour_mean = (sums / jnp.maximum(degree, 1.0)[:, None]).astype(jnp.bfloat16)
    self_rows = jnp.concatenate([title_vectors, encoded[titles:]], axis=0)
    piece = lax.all_gather(sage_weight, "fsdp", axis=1, tiled=True)
    running = jnp.dot(self_rows, piece[0], preferred_element_type=jnp.float32)
    combined = running + jnp.dot(neighbour_mean, piece[1], preferred_element_type=jnp.float32)
    node_output = layer_norm(combined, node_gain).astype(jnp.bfloat16)
    return (title_vectors, node_output)


def solution(mesh):
    return jax.shard_map(
        on_device,
        mesh=mesh,
        in_specs=(
            P(("fsdp", "dom"), None, None),
            P(("fsdp", "dom"), None),
            P("fsdp", None),
            P("fsdp", None),
            P("fsdp", None),
            P("fsdp", None),
            P(),
            P(),
            P(("fsdp", "dom"), None),
            P(("fsdp", "dom"), None, None),
            P(("fsdp", "dom"), None),
            P(("fsdp", "dom"), None, None),
            P(None, "fsdp", None),
            P(),
        ),
        out_specs=(P(("fsdp", "dom"), None), P(("fsdp", "dom"), None)),
        check_vma=False,
    )
```

profile of v0, /device:TPU:0, one launch (start us, length us, event | category | flops | bytes accessed | tf_op | source)
XLA Modules:
  0.0 387.3 jit_solution(11818364927257436339)
XLA Ops:
  11.3 7.3 %all-to-all-start.1 = ((bf16[32,1,1]{2,1,0:T(2,128)(2,1)}), bf16[32,1,1]{2,1,0:T(2,128)(2,1)S(1)}, u32[]{:S(2)}, u32[]{:S(2)}) async-start(bf16[32,1,1]{2,1,0:T(2,128)(2,1)} %copy.50), calls=%async_computation.1 | async-start | bytes 32768 | tf_op jit(solution)/shard_map/all_to_all | solution.py:105
  19.5 5.0 %gather_fusion = bf16[1536,768]{1,0:T(8,128)(2,1)S(1)} fusion(bf16[512,768]{1,0:T(8,128)(2,1)S(1)} %copy-done, s32[2048]{0:T(1024)S(1)} %pad_clamp_fusion), kind=kCustom, calls=%fused_computation | custom fusion | bytes 4724736 | tf_op jit(solution)/shard_map/jit(_take)/gather | solution.py:100
  24.5 1.7 broadcast_select_fusion
  26.2 5.8 %all-to-all-start = ((bf16[32,48,768]{2,1,0:T(8,128)(2,1)}), bf16[32,48,768]{2,1,0:T(8,128)(2,1)S(1)}, u32[]{:S(2)}, u32[]{:S(2)}) async-start(bf16[32,48,768]{2,1,0:T(8,128)(2,1)} %broadcast_select_fusion), calls=%async_computation | async-start | bytes 4718592 | tf_op jit(solution)/shard_map/all_to_all | solution.py:104
  32.7 2.6 copy.54
  36.3 11.1 %scatter_custom_fusion.1 = f32[512]{0:T(512)S(1)} fusion(s32[1536]{0:T(1024)S(1)} %reshape.151, f32[1536]{0:T(1024)S(1)} %reshape.161, f32[]{:T(128)} %constant.42.clone.1), kind=kCustom, calls=%fused_computation.81 | custom fusion | flops 1536 | bytes 2052 | tf_op jit(solution)/shard_map/scatter-add | solution.py:78
  47.5 70.7 %all-to-all-done = bf16[32,48,768]{2,1,0:T(8,128)(2,1)S(1)} async-done(((bf16[32,48,768]{2,1,0:T(8,128)(2,1)}), bf16[32,48,768]{2,1,0:T(8,128)(2,1)S(1)}, u32[]{:S(2)}, u32[]{:S(2)}) %all-to-all-start) | async-done | bytes 2359328 | tf_op jit(solution)/shard_map/all_to_all | solution.py:104
  118.2 12.9 %scatter_custom_fusion = f32[512,768]{1,0:T(8,128)} fusion(s32[1536]{0:T(1024)S(1)} %reshape.151, bf16[1536,768]{1,0:T(8,128)(2,1)S(1)} %bitcast.72, f32[1536]{0:T(1024)S(1)} %reshape.161, f32[]{:T(128)} %constant.42.clone.1), kind=kCustom, calls=%fused_computation.30 | custom fusion | flops 3538944 | bytes 3940356 | tf_op jit(solution)/shard_map/scatter-add | solution.py:77
  131.1 8.5 %convolution_convert_fusion = bf16[1024,2304]{1,0:T(8,128)(2,1)} fusion(bf16[1024,768]{1,0:T(8,128)(2,1)} %bitcast.74, bf16[768,2304]{1,0:T(8,128)(2,1)} %all-gather.6.cloned.1.call-done), kind=kOutput, calls=%fused_computation.27 | convolution fusion | flops 3626237952 | bytes 9830400 | tf_op jit(solution)/shard_map/dot_general | solution.py:35
  139.7 6.7 %copy.42 = bf16[1024,2304]{0,1:T(8,128)(2,1)} copy(bf16[1024,2304]{1,0:T(8,128)(2,1)} %convolution_convert_fusion) | data formatting | bytes 9437184 | tf_op jit(solution)/shard_map/convert_element_type | solution.py:35
  146.4 3.6 copy.58
  150.3 1.0 fusion.26
  151.4 2.6 fusion.70
  154.1 1.0 fusion.27
  155.0 1.2 copy.47
  156.3 2.8 fusion.71
  159.6 1.6 multiply_convert_fusion
  161.1 73.8 %all-gather.10.cloned.1.call-done = bf16[768,3072]{1,0:T(8,128)(2,1)} async-done(((bf16[96,3072]{1,0:T(8,128)(2,1)}), bf16[768,3072]{1,0:T(8,128)(2,1)}) %all-gather.10.cloned.1.call-update) | async-done | bytes 4718608 | tf_op jit(solution)/shard_map/all_gather | solution.py:54
  234.9 79.8 %all-gather.12.cloned.1.call-done = bf16[3072,768]{1,0:T(8,128)(2,1)} async-done(((bf16[384,768]{1,0:T(8,128)(2,1)}), bf16[3072,768]{1,0:T(8,128)(2,1)}) %all-gather.12.cloned.1.call-update) | async-done | bytes 4718608 | tf_op jit(solution)/shard_map/all_gather | solution.py:55
  314.7 51.6 %fusion.72 = (f32[1024]{0:T(1024)S(1)}, f32[1024,768]{0,1:T(8,128)S(1)}) fusion(bf16[3072,768]{1,0:T(8,128)(2,1)} %all-gather.12.cloned.1.call-done, bf16[1024,768]{0,1:T(8,128)(2,1)} %multiply_convert_fusion, bf16[768,3072]{1,0:T(8,128)(2,1)} %all-gather.10.cloned.1.call-done), kind=kOutput, calls=%fused_computation.120 | convolution fusion | flops 9870507008 | bytes 14159872 | tf_op jit(solution)/shard_map/dot_general | solution.py:61
  368.9 6.3 %all-gather.14.cloned.1.call-done = bf16[2,768,1024]{2,1,0:T(8,128)(2,1)} async-done(((bf16[2,96,1024]{2,1,0:T(8,128)(2,1)}), bf16[2,768,1024]{2,1,0:T(8,128)(2,1)}) %all-gather.14.cloned.1.call-update) | async-done | bytes 3145744 | tf_op jit(solution)/shard_map/all_gather | solution.py:124
  375.1 2.5 fusion.25
  377.7 1.2 fusion.73
  379.2 1.3 multiply_convert_fusion.1
  (65 shorter events, 10.3 us)
Async XLA Ops:
  7.2 12.3 %copy-start = (bf16[512,768]{1,0:T(8,128)(2,1)S(1)}, bf16[512,768]{1,0:T(8,128)(2,1)}, u32[]{:S(2)}) copy-start(bf16[512,768]{1,0:T(8,128)(2,1)} %param.22) | copy-start | bytes 2359300
  7.2 123.9 %all-gather.6.cloned.1.call-start = ((), (), s32[]{:S(2)}) async-start(), calls=%async_computation.2 | async-start | bytes 3981312 | tf_op jit(solution)/shard_map/all_gather | solution.py:32
  7.9 148.4 %all-gather.8.cloned.1.call-start = ((), (), s32[]{:S(2)}) async-start(), calls=%async_computation.3 | async-start | bytes 1327104 | tf_op jit(solution)/shard_map/all_gather | solution.py:33
  8.7 226.2 %all-gather.10.cloned.1.call-start = ((), (), s32[]{:S(2)}) async-start(), calls=%async_computation.4 | async-start | bytes 5308416 | tf_op jit(solution)/shard_map/all_gather | solution.py:54
  9.4 305.3 %all-gather.12.cloned.1.call-start = ((), (), s32[]{:S(2)}) async-start(), calls=%async_computation.5 | async-start | bytes 5308416 | tf_op jit(solution)/shard_map/all_gather | solution.py:55
  11.3 14.9 %all-to-all-start.1 = ((bf16[32,1,1]{2,1,0:T(2,128)(2,1)}), bf16[32,1,1]{2,1,0:T(2,128)(2,1)S(1)}, u32[]{:S(2)}, u32[]{:S(2)}) async-start(bf16[32,1,1]{2,1,0:T(2,128)(2,1)} %copy.50), calls=%async_computation.1 | async-start | bytes 32768 | tf_op jit(solution)/shard_map/all_to_all | solution.py:105
  19.5 5.0 %copy-start.3 = (s32[1,32,48]{2,1,0:T(8,128)S(1)}, s32[1,32,48]{2,1,0:T(8,128)}, u32[]{:S(2)}) copy-start(s32[1,32,48]{2,1,0:T(8,128)} %param.23) | copy-start | bytes 18436
  26.2 92.0 %all-to-all-start = ((bf16[32,48,768]{2,1,0:T(8,128)(2,1)}), bf16[32,48,768]{2,1,0:T(8,128)(2,1)S(1)}, u32[]{:S(2)}, u32[]{:S(2)}) async-start(bf16[32,48,768]{2,1,0:T(8,128)(2,1)} %broadcast_select_fusion), calls=%async_computation | async-start | bytes 4718592 | tf_op jit(solution)/shard_map/all_to_all | solution.py:104
  32.1 3.2 copy-start.7
  32.1 3.3 copy-start.4
  32.1 343.0 %all-gather.14.cloned.1.call-start = ((), (), s32[]{:S(2)}) async-start(), calls=%async_computation.6 | async-start | bytes 3538944 | tf_op jit(solution)/shard_map/all_gather | solution.py:124
  154.1 2.3 copy-start.2
  156.3 3.2 copy-start.8
  161.1 205.5 %copy-start.9 = (f32[768]{0:T(1024)S(1)}, f32[768]{0:T(1024)}, u32[]{:S(2)}) copy-start(f32[768]{0:T(1024)} %param.21) | copy-start | bytes 9220
  367.8 7.3 %slice-start = ((bf16[512,768]{1,0:T(8,128)(2,1)}), bf16[504,768]{1,0:T(8,128)(2,1)S(1)}, s32[]{:S(2)}) async-start(bf16[512,768]{1,0:T(8,128)(2,1)} %param.22), calls=%async_computation.7 | async-start | bytes 1548288 | tf_op jit(solution)/shard_map/slice | solution.py:123
  368.7 9.0 %copy-start.1 = (f32[512,768]{1,0:T(8,128)S(1)}, f32[512,768]{1,0:T(8,128)}, u32[]{:S(2)}) copy-start(f32[512,768]{1,0:T(8,128)} %scatter_custom_fusion) | copy-start | bytes 4718596
  368.9 10.0 %copy-start.5 = (bf16[8,768]{1,0:T(8,128)(2,1)}, bf16[8,768]{1,0:T(8,128)(2,1)S(1)}, u32[]{:S(2)}) copy-start(bf16[8,768]{1,0:T(8,128)(2,1)S(1)} %copy.51) | copy-start | bytes 36868
  375.1 2.6 copy-start.10
  377.7 1.6 copy-start.6
Sparse Core Ops, SparseCore 0:
  10.2 103.0 all-gather.5
  115.4 39.1 all-gather.7
  156.9 78.0 all-gather.9
  236.9 77.6 all-gather.11
  316.7 58.3 all-gather.13
where the time goes:
time: 393 us; the launch traced here: 387 us
  waiting for transfers between devices  234 us (60%)
  matrix products  68.7 us (17%)
  other arithmetic  36 us (9%)
  local copies, waits for them, and re-layouts  21.3 us (5%)
  between operations  14.3 us (4%)
  starting transfers between devices  13.4 us (3%)
    all_gather x1, waiting for transfers between devices, encode_titles(): lax.all_gather(down_weight, 'fsdp', axis=0, tiled=True)  79.8 us
    all_gather x1, waiting for transfers between devices, encode_titles(): lax.all_gather(up_weight, 'fsdp', axis=0, tiled=True)  73.8 us
    all_to_all x1, waiting for transfers between devices, on_device(): lax.all_to_all(outgoing, ('fsdp', 'dom'), split_axis=0, concat_axis=0, ti...  70.7 us
    dot_general x1, matrix products, encode_titles(): lowered = jnp.dot(inner, full_down, preferred_element_type=jnp.float32)  51.6 us
    scatter-add x1, other arithmetic, scatter_sums(): sums = jax.ops.segment_sum(rows, label_flat, num_segments=nodes)  12.9 us
    scatter-add x1, other arithmetic, scatter_sums(): degree = jax.ops.segment_sum(mask_flat, label_flat, num_segments=nodes)  11.1 us
    dot_general x1, matrix products, encode_titles(): jnp.dot(flat, full_project, preferred_element_type=jnp.float32)  8.55 us
  transfers between devices with their start and end apart: 7, of which 4 were waited for; matrix products, arithmetic and copies ran while one was open for 31% of the time, Pallas kernels for 0%

commit v1 on v0

--- a/solution.py
+++ b/solution.py
@@ -1,3 +1,4 @@
+import functools
 import math
 import jax
 import jax.numpy as jnp
@@ -7,6 +8,25 @@
 HEADS = 12
 HEAD_DIM = 64
 LN_EPSILON = 1e-12
+
+
+def track_the_numbers(inp, which_axis, on_dim):
+    mat_out = jax.lax.axis_index(which_axis)
+    outcome_arr = jax.lax.axis_size(which_axis)
+    high, carry, built = (outcome_arr, mat_out, inp.shape[on_dim])
+    tray = [dev * high if m == on_dim else dev for m, dev in enumerate(inp.shape)]
+    e_now = lax.dynamic_update_slice_in_dim(
+        jnp.zeros(tray, inp.dtype), inp, carry * built, axis=on_dim
+    )
+    for i in [*range(1, high)]:
+        inp = jax.lax.ppermute(
+            inp, axis_name=which_axis, perm=[(m, (m + 1) % high) for m in range(high)]
+        )
+        e_now = lax.dynamic_update_slice_in_dim(e_now, inp, (carry - i) % high * built, axis=on_dim)
+    return e_now
+
+
+balance_yards = functools.partial(track_the_numbers, which_axis="fsdp", on_dim=0)
 
 
 def layer_norm(values, gain):
@@ -52,7 +72,7 @@
     attended = lax.optimization_barrier(attended)
     full_up, full_down = (
         lax.all_gather(up_weight, "fsdp", axis=0, tiled=True),
-        lax.all_gather(down_weight, "fsdp", axis=0, tiled=True),
+        balance_yards(down_weight),
     )
     inner = jax.nn.gelu(
         jnp.dot(attended, full_up, preferred_element_type=jnp.float32), approximate=False

time: 393 us -> 377 us (0.959)
  waiting for transfers between devices: 234 us -> 204 us
  local copies, waits for them, and re-layouts: 21.3 us -> 38.6 us
  matrix products: 68.7 us -> 56.8 us
  starting transfers between devices: 13.4 us -> 19.7 us
    ppermute x0 -> x7, waiting for transfers between devices: none -> 182 us  [track_the_numbers(): jax.lax.ppermute(inp, axis_name=which_axis, perm=[(m, (m + 1) % high) for...]
    all_gather x1 -> x0, waiting for transfers between devices: 79.8 us -> none  [encode_titles(): lax.all_gather(down_weight, 'fsdp', axis=0, tiled=True)]
    all_gather x1, waiting for transfers between devices: 73.8 us -> 2.44 us  [encode_titles(): lax.all_gather(up_weight, 'fsdp', axis=0, tiled=True)]
    all_to_all x1, waiting for transfers between devices: 70.7 us -> 0.01 us  [on_device(): lax.all_to_all(outgoing, ('fsdp', 'dom'), split_axis=0, concat_axis=0, ti...]
    dynamic_update_slice x0 -> x8, local copies, waits for them, and re-layouts: none -> 12.3 us  [the longest x7 11.4 us: track_the_numbers(): lax.dynamic_update_slice_in_dim(e_now, inp, (carry - i) % high * built, a...]
    dot_general x1, matrix products: 51.6 us -> 39.8 us  [encode_titles(): lowered = jnp.dot(inner, full_down, preferred_element_type=jnp.float32)]
    all_gather x1, waiting for transfers between devices: 6.25 us -> 18 us  [on_device(): piece = lax.all_gather(sage_weight, 'fsdp', axis=1, tiled=True)]
    ppermute x0 -> x7, starting transfers between devices: none -> 6.41 us  [track_the_numbers(): jax.lax.ppermute(inp, axis_name=which_axis, perm=[(m, (m + 1) % high) for...]
  transfers between devices with their start and end apart: 7 -> 13, of which waited for: 4 -> 9; matrix products, arithmetic and copies ran while one was open for 31% -> 33% of each run, Pallas kernels for 0% -> 0%
where the time goes in v1:
time: 377 us; the launch traced here: 370 us
  waiting for transfers between devices  204 us (54%)
  matrix products  56.8 us (15%)
  local copies, waits for them, and re-layouts  38.6 us (10%)
  other arithmetic  35.8 us (9%)
  starting transfers between devices  19.7 us (5%)
  between operations  14.7 us (4%)
    ppermute x7, waiting for transfers between devices, track_the_numbers(): jax.lax.ppermute(inp, axis_name=which_axis, perm=[(m, (m + 1) % high) for...  182 us
    dot_general x1, matrix products, encode_titles(): lowered = jnp.dot(inner, full_down, preferred_element_type=jnp.float32)  39.8 us
    all_gather x1, waiting for transfers between devices, on_device(): piece = lax.all_gather(sage_weight, 'fsdp', axis=1, tiled=True)  18 us
    scatter-add x1, other arithmetic, scatter_sums(): sums = jax.ops.segment_sum(rows, label_flat, num_segments=nodes)  12.7 us
    dynamic_update_slice x7, local copies, waits for them, and re-layouts, track_the_numbers(): lax.dynamic_update_slice_in_dim(e_now, inp, (carry - i) % high * built, a...  11.4 us
    scatter-add x1, other arithmetic, scatter_sums(): degree = jax.ops.segment_sum(mask_flat, label_flat, num_segments=nodes)  11.1 us
    dot_general x1, matrix products, encode_titles(): jnp.dot(flat, full_project, preferred_element_type=jnp.float32)  8.48 us
  transfers between devices with their start and end apart: 13, of which 9 were waited for; matrix products, arithmetic and copies ran while one was open for 33% of the time, Pallas kernels for 0%

profile of v1, /device:TPU:0, one launch (start us, length us, event | category | flops | bytes accessed | tf_op | source)
XLA Modules:
  0.0 369.7 jit_solution(4443884126761243739)
XLA Ops:
  10.8 7.3 %all-to-all-start.1 = ((bf16[32,1,1]{2,1,0:T(2,128)(2,1)}), bf16[32,1,1]{2,1,0:T(2,128)(2,1)S(1)}, u32[]{:S(2)}, u32[]{:S(2)}) async-start(bf16[32,1,1]{2,1,0:T(2,128)(2,1)} %copy.50), calls=%async_computation.1 | async-start | bytes 32768 | tf_op jit(solution)/shard_map/all_to_all | solution.py:125
  18.9 5.0 %gather_fusion = bf16[1536,768]{1,0:T(8,128)(2,1)S(1)} fusion(bf16[512,768]{1,0:T(8,128)(2,1)S(1)} %copy-done, s32[2048]{0:T(1024)S(1)} %pad_clamp_fusion), kind=kCustom, calls=%fused_computation | custom fusion | bytes 4724736 | tf_op jit(solution)/shard_map/jit(_take)/gather | solution.py:120
  25.7 5.8 %all-to-all-start = ((bf16[32,48,768]{2,1,0:T(8,128)(2,1)}), bf16[32,48,768]{2,1,0:T(8,128)(2,1)S(1)}, u32[]{:S(2)}, u32[]{:S(2)}) async-start(bf16[32,48,768]{2,1,0:T(8,128)(2,1)} %broadcast_select_fusion), calls=%async_computation | async-start | bytes 4718592 | tf_op jit(solution)/shard_map/all_to_all | solution.py:124
  33.4 86.7 %collective-permute-done = bf16[384,768]{1,0:T(8,128)(2,1)S(1)} collective-permute-done((bf16[384,768]{1,0:T(8,128)(2,1)}, bf16[384,768]{1,0:T(8,128)(2,1)S(1)}, u32[]{:S(2)}, u32[]{:S(2)}) %collective-permute-start) | collective-permute-done | bytes 589856 | tf_op jit(solution)/shard_map/ppermute | solution.py:22
  120.9 17.0 %collective-permute-done.1 = bf16[384,768]{1,0:T(8,128)(2,1)S(1)} collective-permute-done((bf16[384,768]{1,0:T(8,128)(2,1)S(1)}, bf16[384,768]{1,0:T(8,128)(2,1)S(1)}, u32[]{:S(2)}, u32[]{:S(2)}) %collective-permute-start.1) | collective-permute-done | bytes 589856 | tf_op jit(solution)/shard_map/ppermute | solution.py:22
  138.7 20.5 %collective-permute-done.2 = bf16[384,768]{1,0:T(8,128)(2,1)S(1)} collective-permute-done((bf16[384,768]{1,0:T(8,128)(2,1)S(1)}, bf16[384,768]{1,0:T(8,128)(2,1)S(1)}, u32[]{:S(2)}, u32[]{:S(2)}) %collective-permute-start.2) | collective-permute-done | bytes 589856 | tf_op jit(solution)/shard_map/ppermute | solution.py:22
  160.0 2.6 collective-permute-start.3
  162.6 11.7 %collective-permute-done.3 = bf16[384,768]{1,0:T(8,128)(2,1)} collective-permute-done((bf16[384,768]{1,0:T(8,128)(2,1)S(1)}, bf16[384,768]{1,0:T(8,128)(2,1)}, u32[]{:S(2)}, u32[]{:S(2)}) %collective-permute-start.3) | collective-permute-done | bytes 589856 | tf_op jit(solution)/shard_map/ppermute | solution.py:22
  176.4 2.7 copy.54
  179.3 2.5 broadcast_in_dim.30
  182.8 20.8 %collective-permute-done.4 = bf16[384,768]{1,0:T(8,128)(2,1)} collective-permute-done((bf16[384,768]{1,0:T(8,128)(2,1)}, bf16[384,768]{1,0:T(8,128)(2,1)}, u32[]{:S(2)}, u32[]{:S(2)}) %collective-permute-start.4) | collective-permute-done | bytes 589856 | tf_op jit(solution)/shard_map/ppermute | solution.py:22
  204.4 11.1 %scatter_custom_fusion.1 = f32[512]{0:T(512)S(1)} fusion(s32[1536]{0:T(1024)S(1)} %reshape.151, f32[1536]{0:T(1024)S(1)} %reshape.161, f32[]{:T(128)} %constant.56.clone.1), kind=kCustom, calls=%fused_computation.89 | custom fusion | flops 1536 | bytes 2052 | tf_op jit(solution)/shard_map/scatter-add | solution.py:98
  217.5 5.8 %collective-permute-done.5 = bf16[384,768]{1,0:T(8,128)(2,1)S(1)} collective-permute-done((bf16[384,768]{1,0:T(8,128)(2,1)}, bf16[384,768]{1,0:T(8,128)(2,1)S(1)}, u32[]{:S(2)}, u32[]{:S(2)}) %collective-permute-start.5) | collective-permute-done | bytes 589856 | tf_op jit(solution)/shard_map/ppermute | solution.py:22
  231.9 19.0 %collective-permute-done.6 = bf16[384,768]{1,0:T(8,128)(2,1)S(1)} collective-permute-done((bf16[384,768]{1,0:T(8,128)(2,1)S(1)}, bf16[384,768]{1,0:T(8,128)(2,1)S(1)}, u32[]{:S(2)}, u32[]{:S(2)}) %collective-permute-start.6) | collective-permute-done | bytes 589856 | tf_op jit(solution)/shard_map/ppermute | solution.py:22
  251.8 12.7 %scatter_custom_fusion = f32[512,768]{1,0:T(8,128)} fusion(s32[1536]{0:T(1024)S(1)} %reshape.151, bf16[1536,768]{1,0:T(8,128)(2,1)S(1)} %bitcast.72, f32[1536]{0:T(1024)S(1)} %reshape.161, f32[]{:T(128)} %constant.56.clone.1), kind=kCustom, calls=%fused_computation.30 | custom fusion | flops 3538944 | bytes 3940356 | tf_op jit(solution)/shard_map/scatter-add | solution.py:97
  264.5 8.5 %convolution_convert_fusion = bf16[1024,2304]{1,0:T(8,128)(2,1)} fusion(bf16[1024,768]{1,0:T(8,128)(2,1)} %bitcast.74, bf16[768,2304]{1,0:T(8,128)(2,1)} %all-gather.5.cloned.1.call-done), kind=kOutput, calls=%fused_computation.27 | convolution fusion | flops 3626237952 | bytes 9830400 | tf_op jit(solution)/shard_map/dot_general | solution.py:55
  273.0 6.7 %copy.42 = bf16[1024,2304]{0,1:T(8,128)(2,1)} copy(bf16[1024,2304]{1,0:T(8,128)(2,1)} %convolution_convert_fusion) | data formatting | bytes 9437184 | tf_op jit(solution)/shard_map/convert_element_type | solution.py:55
  279.6 3.6 copy.58
  284.6 2.6 fusion.70
  289.6 2.8 fusion.71
  294.4 2.4 all-gather.9.cloned.1.call-done
  296.8 39.8 %fusion.72 = (f32[1024]{0:T(1024)S(1)}, f32[1024,768]{0,1:T(8,128)S(1)}) fusion(bf16[3072,768]{1,0:T(8,128)(2,1)} %constant_dynamic-update-slice_fusion, bf16[1024,768]{0,1:T(8,128)(2,1)} %multiply_convert_fusion, bf16[768,3072]{1,0:T(8,128)(2,1)} %all-gather.9.cloned.1.call-done), kind=kOutput, calls=%fused_computation.128 | convolution fusion | flops 9870507008 | bytes 14159872 | tf_op jit(solution)/shard_map/dot_general | solution.py:81
  339.3 18.0 %all-gather.11.cloned.1.call-done = bf16[2,768,1024]{2,1,0:T(8,128)(2,1)} async-done(((bf16[2,96,1024]{2,1,0:T(8,128)(2,1)}), bf16[2,768,1024]{2,1,0:T(8,128)(2,1)}) %all-gather.11.cloned.1.call-update) | async-done | bytes 3145744 | tf_op jit(solution)/shard_map/all_gather | solution.py:144
  357.3 2.5 fusion.25
  (93 shorter events, 36.8 us)
Async XLA Ops:
  7.2 11.7 %copy-start = (bf16[512,768]{1,0:T(8,128)(2,1)S(1)}, bf16[512,768]{1,0:T(8,128)(2,1)}, u32[]{:S(2)}) copy-start(bf16[512,768]{1,0:T(8,128)(2,1)} %param.22) | copy-start | bytes 2359300
  7.2 257.3 %all-gather.5.cloned.1.call-start = ((), (), s32[]{:S(2)}) async-start(), calls=%async_computation.2 | async-start | bytes 3981312 | tf_op jit(solution)/shard_map/all_gather | solution.py:52
  7.9 281.6 %all-gather.7.cloned.1.call-start = ((), (), s32[]{:S(2)}) async-start(), calls=%async_computation.3 | async-start | bytes 1327104 | tf_op jit(solution)/shard_map/all_gather | solution.py:53
  8.7 288.2 %all-gather.9.cloned.1.call-start = ((), (), s32[]{:S(2)}) async-start(), calls=%async_computation.4 | async-start | bytes 5308416 | tf_op jit(solution)/shard_map/all_gather | solution.py:74
  10.8 14.9 %all-to-all-start.1 = ((bf16[32,1,1]{2,1,0:T(2,128)(2,1)}), bf16[32,1,1]{2,1,0:T(2,128)(2,1)S(1)}, u32[]{:S(2)}, u32[]{:S(2)}) async-start(bf16[32,1,1]{2,1,0:T(2,128)(2,1)} %copy.50), calls=%async_computation.1 | async-start | bytes 32768 | tf_op jit(solution)/shard_map/all_to_all | solution.py:125
  18.9 5.0 %copy-start.7 = (s32[1,32,48]{2,1,0:T(8,128)S(1)}, s32[1,32,48]{2,1,0:T(8,128)}, u32[]{:S(2)}) copy-start(s32[1,32,48]{2,1,0:T(8,128)} %param.23) | copy-start | bytes 18436
  25.7 153.4 %copy-start.11 = (s32[8,128]{1,0:T(8,128)S(1)}, s32[8,128]{1,0:T(8,128)}, u32[]{:S(2)}) copy-start(s32[8,128]{1,0:T(8,128)} %param.15) | copy-start | bytes 12292
  25.7 153.6 %copy-start.8 = (s32[1,32,48]{2,1,0:T(8,128)S(1)}, s32[1,32,48]{2,1,0:T(8,128)}, u32[]{:S(2)}) copy-start(s32[1,32,48]{2,1,0:T(8,128)} %param.25) | copy-start | bytes 18436
  25.7 226.1 %all-to-all-start = ((bf16[32,48,768]{2,1,0:T(8,128)(2,1)}), bf16[32,48,768]{2,1,0:T(8,128)(2,1)S(1)}, u32[]{:S(2)}, u32[]{:S(2)}) async-start(bf16[32,48,768]{2,1,0:T(8,128)(2,1)} %broadcast_select_fusion), calls=%async_computation | async-start | bytes 4718592 | tf_op jit(solution)/shard_map/all_to_all | solution.py:124
  31.5 325.8 %all-gather.11.cloned.1.call-start = ((), (), s32[]{:S(2)}) async-start(), calls=%async_computation.5 | async-start | bytes 3538944 | tf_op jit(solution)/shard_map/all_gather | solution.py:144
  31.6 88.5 %collective-permute-start = (bf16[384,768]{1,0:T(8,128)(2,1)}, bf16[384,768]{1,0:T(8,128)(2,1)S(1)}, u32[]{:S(2)}, u32[]{:S(2)}) collective-permute-start(bf16[384,768]{1,0:T(8,128)(2,1)} %param.19), channel_id=1, source_target_pairs={{0,4},{4,8},{8,12},{12,16},{16,20},{20,24},{24,28},{28,0},{1,5},{5... | collective-permute-start | bytes 1769480 | tf_op jit(solution)/shard_map/ppermute | solution.py:22
  120.1 17.8 %collective-permute-start.1 = (bf16[384,768]{1,0:T(8,128)(2,1)S(1)}, bf16[384,768]{1,0:T(8,128)(2,1)S(1)}, u32[]{:S(2)}, u32[]{:S(2)}) collective-permute-start(bf16[384,768]{1,0:T(8,128)(2,1)S(1)} %collective-permute-done), channel_id=1, source_target_pairs={{0,4},{4,8},{8,12},{12,16},{16,20},{20,24},{24,28},{28,0},{1,5},{5... | collective-permute-start | bytes 1769480 | tf_op jit(solution)/shard_map/ppermute | solution.py:22
  138.7 20.5 %collective-permute-start.2 = (bf16[384,768]{1,0:T(8,128)(2,1)S(1)}, bf16[384,768]{1,0:T(8,128)(2,1)S(1)}, u32[]{:S(2)}, u32[]{:S(2)}) collective-permute-start(bf16[384,768]{1,0:T(8,128)(2,1)S(1)} %collective-permute-done.1), channel_id=1, source_target_pairs={{0,4},{4,8},{8,12},{12,16},{16,20},{20,24},{24,28},{28,0},{1,5},{5... | collective-permute-start | bytes 1769480 | tf_op jit(solution)/shard_map/ppermute | solution.py:22
  160.0 14.2 %collective-permute-start.3 = (bf16[384,768]{1,0:T(8,128)(2,1)S(1)}, bf16[384,768]{1,0:T(8,128)(2,1)}, u32[]{:S(2)}, u32[]{:S(2)}) collective-permute-start(bf16[384,768]{1,0:T(8,128)(2,1)S(1)} %collective-permute-done.2), channel_id=1, source_target_pairs={{0,4},{4,8},{8,12},{12,16},{16,20},{20,24},{24,28},{28,0},{1,5},{5... | collective-permute-start | bytes 1769480 | tf_op jit(solution)/shard_map/ppermute | solution.py:22
  174.3 29.3 %collective-permute-start.4 = (bf16[384,768]{1,0:T(8,128)(2,1)}, bf16[384,768]{1,0:T(8,128)(2,1)}, u32[]{:S(2)}, u32[]{:S(2)}) collective-permute-start(bf16[384,768]{1,0:T(8,128)(2,1)} %collective-permute-done.3), channel_id=1, source_target_pairs={{0,4},{4,8},{8,12},{12,16},{16,20},{20,24},{24,28},{28,0},{1,5},{5... | collective-permute-start | bytes 1769480 | tf_op jit(solution)/shard_map/ppermute | solution.py:22
  176.4 5.5 %copy-start.3 = (bf16[384,768]{1,0:T(8,128)(2,1)S(1)}, bf16[384,768]{1,0:T(8,128)(2,1)}, u32[]{:S(2)}) copy-start(bf16[384,768]{1,0:T(8,128)(2,1)} %param.19) | copy-start | bytes 1769476
  203.6 19.7 %collective-permute-start.5 = (bf16[384,768]{1,0:T(8,128)(2,1)}, bf16[384,768]{1,0:T(8,128)(2,1)S(1)}, u32[]{:S(2)}, u32[]{:S(2)}) collective-permute-start(bf16[384,768]{1,0:T(8,128)(2,1)} %collective-permute-done.4), channel_id=1, source_target_pairs={{0,4},{4,8},{8,12},{12,16},{16,20},{20,24},{24,28},{28,0},{1,5},{5... | collective-permute-start | bytes 1769480 | tf_op jit(solution)/shard_map/ppermute | solution.py:22
  223.3 27.6 %collective-permute-start.6 = (bf16[384,768]{1,0:T(8,128)(2,1)S(1)}, bf16[384,768]{1,0:T(8,128)(2,1)S(1)}, u32[]{:S(2)}, u32[]{:S(2)}) collective-permute-start(bf16[384,768]{1,0:T(8,128)(2,1)S(1)} %collective-permute-done.5), channel_id=1, source_target_pairs={{0,4},{4,8},{8,12},{12,16},{16,20},{20,24},{24,28},{28,0},{1,5},{5... | collective-permute-start | bytes 1769480 | tf_op jit(solution)/shard_map/ppermute | solution.py:22
  289.6 3.2 copy-start.12
  294.4 42.6 %copy-start.13 = (f32[768]{0:T(1024)S(1)}, f32[768]{0:T(1024)}, u32[]{:S(2)}) copy-start(f32[768]{0:T(1024)} %param.21) | copy-start | bytes 9220
  337.4 19.9 %slice-start = ((bf16[512,768]{1,0:T(8,128)(2,1)}), bf16[504,768]{1,0:T(8,128)(2,1)S(1)}, s32[]{:S(2)}) async-start(bf16[512,768]{1,0:T(8,128)(2,1)} %param.22), calls=%async_computation.6 | async-start | bytes 1548288 | tf_op jit(solution)/shard_map/slice | solution.py:143
  338.2 21.6 %copy-start.2 = (f32[512,768]{1,0:T(8,128)S(1)}, f32[512,768]{1,0:T(8,128)}, u32[]{:S(2)}) copy-start(f32[512,768]{1,0:T(8,128)} %scatter_custom_fusion) | copy-start | bytes 4718596
  339.3 21.8 %copy-start.9 = (bf16[8,768]{1,0:T(8,128)(2,1)}, bf16[8,768]{1,0:T(8,128)(2,1)S(1)}, u32[]{:S(2)}) copy-start(bf16[8,768]{1,0:T(8,128)(2,1)S(1)} %copy.51) | copy-start | bytes 36868
  357.3 2.6 copy-start.14
  (5 other events, 6.3 us)
Sparse Core Ops, SparseCore 0:
  10.2 103.0 all-gather.4
  115.4 82.3 all-gather.6
  200.0 96.7 all-gather.8
  298.9 58.3 all-gather.10
